TPU v7x, 32 devices: a whole 2x2x4 slice. The times are simulated.
32 devices in a mesh: obs: 2 (over y), bt: 4 (over z), freq: 2 (over x), pol: 2 (over core).
Axes of the slice: x: 2, y: 2, z: 4, core: 2. Of those that a mesh axis runs over, the one named last changes fastest.
Arguments:
- gains: float32 [16, 4, 8, 1984], P(('obs', 'bt', 'pol'), 'freq'), parts along dimension 0, may hold values from -3 to 3
- visibilities: bfloat16 [16, 4, 8, 4096], P('obs', 'freq', None, ('bt', 'pol')), parts along dimension 0, may hold values from -6 to 6
- first_station: int32 [8192], P(('obs', 'bt', 'pol')), parts along dimension 0, may hold values from 0 to 61
- second_station: int32 [8192], P(('obs', 'bt', 'pol')), parts along dimension 0, may hold values from 0 to 61, as said below
- filled_row_count: int32 [16], P(('obs', 'bt', 'pol')), parts along dimension 0, may hold values from 256 to 512
- facet_dir: int32 [16], P('obs'), parts along dimension 0, may hold values from 0 to 7, each once
Outputs:
- corrected: bfloat16 [16, 4, 8, 4096], P('obs', 'freq', None, ('bt', 'pol')), parts along dimension 0
There are 2 independent parts, one for each index of `obs`. A program takes and returns all parts, laid end to end along the dimension named above; each array names one. Nothing has to cross between parts.
Inputs may be any that keep to these rules, and one draw needn't show every extreme that they name: In every row second_station differs from first_station. `facet_dir`: each direction names exactly one facet.
All inputs are finite; a program needn't handle non-finite values.
Results may differ from a plain program's by a relative error of at most 0.001.
Values sent between devices are 32-bit elements; how exact they have to be, the bound alone decides.
A program may use at most 64 MiB of HBM per device.

v0:
```python
import functools

import jax
import jax.numpy as jnp
from jax import lax
from jax.experimental import pallas as pl
from jax.experimental.pallas import tpu as pltpu
from jax.sharding import PartitionSpec as P

ARRAY_STATIONS = 62
GAIN_SLOT_COUNT = 4
MESH = pl.DeviceIdType.MESH
LANES = 128
HALF = 64
COMPS = 8
F32 = jnp.float32
BF16 = jnp.bfloat16


def pair_tile(left, right):
    gap = jnp.zeros((left.shape[0], HALF - ARRAY_STATIONS), F32)
    return jnp.concatenate([left, gap, right, gap], axis=1)


def complex_dot(pairs, conj):
    re = im = None
    for (ar, ai), (br, bi) in pairs:
        if conj:
            pr = ar * br + ai * bi
            pi = ai * br - ar * bi
        else:
            pr = ar * br - ai * bi
            pi = ar * bi + ai * br
        re = pr if re is None else re + pr
        im = pi if im is None else im + pi
    return re, im


def jones(left, data, right):
    a = lambda m, i, j: (m[2 * i + j], m[4 + 2 * i + j])
    mid = {}
    for i in (0, 1):
        for j in (0, 1):
            mid[i, j] = complex_dot(
                [(a(left, i, t), a(data, t, j)) for t in (0, 1)], False
            )
    out = [None] * COMPS
    for i in (0, 1):
        for j in (0, 1):
            re, im = complex_dot(
                [(mid[i, t], a(right, j, t)) for t in (0, 1)], True
            )
            out[2 * i + j], out[4 + 2 * i + j] = re, im
    return out


def kernel(
    n,
    pols,
    gains_hbm,
    vis_hbm,
    first_hbm,
    second_hbm,
    filled_hbm,
    dir_hbm,
    out_ref,
    gains,
    vis,
    stations,
    filled,
    dirs,
    send,
    recv,
    table,
    planar,
    in_sem,
    send_sem,
    recv_sem,
):
    facets, chans, comps, rows = vis.shape
    slots = GAIN_SLOT_COUNT
    per_slot = rows // slots
    tiles = send.shape[0] // COMPS // n
    ck = chans * comps
    bts = n // pols
    my_bt, my_pol = lax.axis_index("bt"), lax.axis_index("pol")
    me = my_bt * pols + my_pol
    steps = [(dz, dp) for dz in range(bts) for dp in range(pols) if dz or dp]
    steps.sort(key=lambda step: (step[0] == 0, abs(2 * step[0] - bts)))
    peers = [
        (lax.rem(my_bt + dz, bts), lax.rem(my_pol + dp, pols)) for dz, dp in steps
    ]

    copies = [
        pltpu.make_async_copy(src, dst, in_sem.at[i])
        for src, dst, i in [
            (gains_hbm, gains, 0),
            (first_hbm, stations.at[0], 1),
            (second_hbm, stations.at[1], 1),
            (dir_hbm, dirs, 2),
            (filled_hbm, filled, 3),
            (vis_hbm, vis, 4),
        ]
    ]
    copies[0].start()
    barrier = pltpu.get_barrier_semaphore()
    for bt, pol in peers:
        pl.semaphore_signal(
            barrier, inc=1, device_id={"bt": bt, "pol": pol}, device_id_type=MESH
        )
    for copy in copies[1:]:
        copy.start()

    copies[0].wait()
    lane = lax.broadcasted_iota(jnp.int32, (COMPS, LANES), 1)
    st = ARRAY_STATIONS

    def slot_of(c, t):
        t = min(t, n * slots - 1)
        return gains[0, c, :, t * st : (t + 1) * st]

    for b in range(n):
        at = 0
        for pair in range(slots // 2):
            for c in range(chans):
                t = b * slots + 2 * pair
                send[pl.ds((b * tiles + at) * COMPS, COMPS), :] = pair_tile(
                    slot_of(c, t), slot_of(c, t + 1)
                )
                at += 1
        for c in range(0, chans, 2):
            t = (b + 1) * slots
            send[pl.ds((b * tiles + at) * COMPS, COMPS), :] = pair_tile(
                slot_of(c, t), slot_of(min(c + 1, chans - 1), t)
            )
            at += 1

    pl.semaphore_wait(barrier, n - 1)
    slab = tiles * COMPS

    mine = pl.ds(pl.multiple_of(me * slab, 8), slab)
    for bt, pol in peers:
        pltpu.make_async_remote_copy(
            src_ref=send.at[pl.ds(pl.multiple_of((bt * pols + pol) * slab, 8), slab), :],
            dst_ref=recv.at[mine, :],
            send_sem=send_sem,
            recv_sem=recv_sem,
            device_id={"bt": bt, "pol": pol},
            device_id_type=MESH,
        ).start()
    recv[mine, :] = send[mine, :]

    pltpu.make_async_copy(stations, stations, in_sem.at[1]).wait()
    copies[3].wait()
    copies[4].wait()
    row = lax.broadcasted_iota(jnp.int32, (LANES, per_slot), 0)
    col = lax.broadcasted_iota(jnp.int32, (LANES, per_slot), 1)
    station = lax.rem(row, HALF)
    lower = row < HALF
    frac = (col.astype(F32) + 0.5) / per_slot
    live_rows = filled[0]
    for s in range(slots):
        now, then = 1.0 - frac, frac
        weight = jnp.where(lower, now, then) if s % 2 == 0 else jnp.where(lower, then, now)
        live = (col + s * per_slot) < live_rows
        first = stations[0, s : s + 1, :]
        second = stations[1, s : s + 1, :]
        lt = jnp.where((station == first) & live, weight, 0.0)
        rt = jnp.where(station == second, weight, 0.0)
        both = jnp.concatenate([lt, rt], axis=1).astype(BF16)
        table[s, 0:LANES, :] = both
        table[s, LANES : 2 * LANES, :] = both

    copies[5].wait()
    total = facets * ck
    prow = lax.broadcasted_iota(jnp.int32, (total, total), 0)
    pcol = lax.broadcasted_iota(jnp.int32, (total, total), 1)
    facet_of = pcol // ck
    dir_of = jnp.zeros_like(pcol)
    for f in range(facets):
        dir_of = jnp.where(facet_of == f, dirs[f], dir_of)
    target = lax.rem(pcol, ck) * facets + dir_of
    perm32 = jnp.where(prow == target, 1.0, 0.0)
    perm = perm32.astype(BF16)
    unperm = perm32.T.astype(BF16)
    flat = vis[...].astype(F32).reshape(total, rows).astype(BF16)
    planar[...] = jnp.dot(perm, flat, preferred_element_type=F32)

    arrived = recv.at[pl.ds(0, (n - 1) * slab), :]
    pltpu.make_async_copy(arrived, arrived, recv_sem).wait()

    def gathered(at, c_rot):
        planes = []
        for k in range(comps):
            plane = recv[pl.ds(at * COMPS + k, facets, stride=slab), :]
            if c_rot:
                plane = pltpu.roll(plane, HALF, 1)
            planes.append(plane)
        return planes

    def stacked(pair):
        planes = []
        for c in range(chans):
            if pair < slots // 2:
                planes += gathered(pair * chans + c, False)
            else:
                planes += gathered((slots // 2) * chans + c // 2, c % 2 == 1)
        return jnp.concatenate(planes, axis=0)

    pairs = [stacked(p) for p in range(slots // 2 + 1)]
    in_low = lax.broadcasted_iota(jnp.int32, (total, LANES), 1) < HALF
    done = []
    for s in range(slots):
        made = []
        x = pairs[s // 2]
        if s % 2 == 1:
            x = jnp.where(in_low, pairs[s // 2 + 1], x)
        hi = x.astype(BF16)
        lo = (x - hi.astype(F32)).astype(BF16)
        spread = jnp.dot(
            jnp.concatenate([hi, lo], axis=1), table[s], preferred_element_type=F32
        )
        for c in range(chans):
            take = lambda k: slice((c * comps + k) * facets, (c * comps + k + 1) * facets)
            left = [spread[take(k), 0:per_slot] for k in range(comps)]
            right = [spread[take(k), per_slot:] for k in range(comps)]
            data = [planar[take(k), s * per_slot : (s + 1) * per_slot] for k in range(comps)]
            made += jones(left, data, right)
        done.append(jnp.concatenate(made, axis=0).astype(BF16))
        if s % 2 == 1:
            wide = jnp.concatenate(done, axis=1)
            done = []
            back = jnp.dot(unperm, wide, preferred_element_type=F32)
            for f in range(facets):
                for c in range(chans):
                    at = (f * chans + c) * comps
                    out_ref[f, c, :, (s - 1) * per_slot : (s + 1) * per_slot] = back[
                        at : at + comps, :
                    ].astype(BF16)

    sent = send.at[pl.ds(0, (n - 1) * slab), :]
    pltpu.make_async_copy(sent, sent, send_sem).wait()


def shards(gains, visibilities, first_station, second_station, filled_row_count, facet_dir):
    n = lax.axis_size(("bt", "pol"))
    pols = lax.axis_size("pol")
    facets, chans, comps, rows = visibilities.shape
    slots = GAIN_SLOT_COUNT
    tiles = (slots // 2) * chans + (chans + 1) // 2
    total = facets * chans * comps
    anywhere = pl.BlockSpec(memory_space=pltpu.HBM)
    return pl.pallas_call(
        functools.partial(kernel, n, pols),
        out_shape=pltpu.VMEM(visibilities.shape, BF16),
        in_specs=[anywhere] * 6,
        out_specs=pl.BlockSpec(memory_space=pltpu.VMEM),
        scratch_shapes=[
            pltpu.VMEM(gains.shape, F32),
            pltpu.VMEM(visibilities.shape, BF16),
            pltpu.VMEM((2, slots, rows // slots), jnp.int32),
            pltpu.SMEM(filled_row_count.shape, jnp.int32),
            pltpu.SMEM(facet_dir.shape, jnp.int32),
            pltpu.VMEM((n * tiles * COMPS, LANES), F32),
            pltpu.VMEM((n * tiles * COMPS, LANES), F32),
            pltpu.VMEM((slots, 2 * LANES, 2 * (rows // slots)), BF16),
            pltpu.VMEM((total, rows), F32),
            pltpu.SemaphoreType.DMA((5,)),
            pltpu.SemaphoreType.DMA,
            pltpu.SemaphoreType.DMA,
        ],
        compiler_params=pltpu.CompilerParams(collective_id=0, has_side_effects=True),
        name="jones",
    )(
        gains,
        visibilities,
        first_station.reshape(slots, rows // slots),
        second_station.reshape(slots, rows // slots),
        filled_row_count,
        facet_dir,
    )


def solution(mesh):
    return jax.shard_map(
        shards,
        mesh=mesh,
        in_specs=(
            P(("obs", "bt", "pol"), "freq", None, None),
            P("obs", "freq", None, ("bt", "pol")),
            P(("obs", "bt", "pol")),
            P(("obs", "bt", "pol")),
            P(("obs", "bt", "pol")),
            P("obs"),
        ),
        out_specs=P("obs", "freq", None, ("bt", "pol")),
        check_vma=False,
    )
```

profile of v0, /device:TPU:0, one launch (start us, length us, event | category | flops | bytes accessed | tf_op | source)
XLA Modules:
  0.0 11.1 jit_solution(14578240336828323102)
XLA Ops:
  0.7 9.8 %jones.1 = bf16[8,2,8,512]{3,2,1,0:T(8,128)(2,1)S(1)} custom-call(f32[1,2,8,1984]{3,2,1,0:T(8,128)} %gains_hbm.1, bf16[8,2,8,512]{3,2,1,0:T(8,128)(2,1)} %vis_hbm.1, s32[4,128]{1,0:T(4,128)} %bitcast.2, s32[4,128]{1,0:T(4,128)} %bitcast.3, s32[1]{0:T(128)S(6)} %copy.9.filled_hbm, s32[8]{0:T(128)} %dir_hbm.1), custom_call_target="tpu_custom_call" | custom-call | tf_op jit(solution)/shard_map/jones/pallas_call | solution.py:253
  10.5 0.7 %copy.8 = bf16[8,2,8,512]{3,2,1,0:T(8,128)(2,1)} copy(bf16[8,2,8,512]{3,2,1,0:T(8,128)(2,1)S(1)} %jones.1) | data formatting | bytes 262144
where the time goes:
time: 11.3 us; the launch traced here: 11.1 us
  Pallas kernels  9.82 us (87%)
  local copies, waits for them, and re-layouts  0.66 us (6%)
  between operations  0.66 us (6%)
    pallas_call x1, Pallas kernels, shards(): pl.pallas_call(functools.partial(kernel, n, pols), out_shape=pltpu.VMEM(v...  9.82 us
    unnamed x1, local copies, waits for them, and re-layouts  0.66 us

commit v1 on v0

v1 whole, which is shorter than its diff:
```python
import functools

import jax
import jax.numpy as jnp
from jax import lax
from jax.experimental import pallas as pl
from jax.experimental.pallas import tpu as pltpu
from jax.sharding import PartitionSpec as P

ARRAY_STATIONS = 62
GAIN_SLOT_COUNT = 4
MESH = pl.DeviceIdType.MESH
LANES = 128
HALF = 64
COMPS = 8
F32 = jnp.float32
BF16 = jnp.bfloat16


def complex_dot(pairs, conj):
    re = im = None
    for (ar, ai), (br, bi) in pairs:
        if conj:
            pr = ar * br + ai * bi
            pi = ai * br - ar * bi
        else:
            pr = ar * br - ai * bi
            pi = ar * bi + ai * br
        re = pr if re is None else re + pr
        im = pi if im is None else im + pi
    return re, im


def jones(left, data, right):
    a = lambda m, i, j: (m[2 * i + j], m[4 + 2 * i + j])
    mid = {}
    for i in (0, 1):
        for j in (0, 1):
            mid[i, j] = complex_dot(
                [(a(left, i, t), a(data, t, j)) for t in (0, 1)], False
            )
    out = [None] * COMPS
    for i in (0, 1):
        for j in (0, 1):
            re, im = complex_dot(
                [(mid[i, t], a(right, j, t)) for t in (0, 1)], True
            )
            out[2 * i + j], out[4 + 2 * i + j] = re, im
    return out


def pack(gains, send, n, targets):
    slots, st = GAIN_SLOT_COUNT, ARRAY_STATIONS
    chans = gains.shape[1]
    pitch = slots // 2 * COMPS + COMPS // 2
    half = COMPS // 2
    gap8 = jnp.zeros((COMPS, HALF - st), F32)
    gap4 = jnp.zeros((half, HALF - st), F32)

    def slot_of(c, t):
        t = min(t, n * slots - 1)
        return gains[0, c, :, t * st : (t + 1) * st]

    for b in targets:
        for c in range(chans):
            at = (b * chans + c) * pitch
            for pair in range(slots // 2):
                t = b * slots + 2 * pair
                send[at + pair * COMPS : at + (pair + 1) * COMPS, :] = jnp.concatenate(
                    [slot_of(c, t), gap8, slot_of(c, t + 1), gap8], axis=1
                )
            last = slot_of(c, (b + 1) * slots)
            at += slots // 2 * COMPS
            send[at : at + half, :] = jnp.concatenate(
                [last[:half], gap4, last[half:], gap4], axis=1
            )


def kernel(
    n,
    pols,
    gains_hbm,
    vis_hbm,
    first_hbm,
    second_hbm,
    filled_hbm,
    dir_hbm,
    out_ref,
    gains,
    vis,
    stations,
    filled,
    dirs,
    send,
    recv,
    planar,
    stage,
    table,
    in_sem,
    send_sem,
    recv_sem,
    ready,
):
    facets, chans, comps, rows = vis.shape
    slots = GAIN_SLOT_COUNT
    per_slot = rows // slots
    pitch = slots // 2 * COMPS + COMPS // 2
    slab = chans * pitch
    group = COMPS // chans
    bts = n // pols
    my_bt, my_pol = lax.axis_index("bt"), lax.axis_index("pol")
    me = my_bt * pols + my_pol
    everyone = [(b, p) for b in range(bts) for p in range(pols)]

    copies = [
        pltpu.make_async_copy(src, dst, in_sem.at[i])
        for src, dst, i in [
            (gains_hbm, gains, 0),
            (first_hbm, stations.at[0], 1),
            (second_hbm, stations.at[1], 1),
            (dir_hbm, dirs, 2),
            (filled_hbm, filled, 3),
            (vis_hbm, vis, 4),
        ]
    ]
    copies[0].start()
    barrier = pltpu.get_barrier_semaphore()
    for b, p in everyone:
        mate = jnp.logical_and(my_bt == b, my_pol != p)

        @pl.when(jnp.logical_or(my_bt < b, mate))
        def _():
            pl.semaphore_signal(
                barrier, inc=1, device_id={"bt": b, "pol": p}, device_id_type=MESH
            )

    for copy in copies[1:]:
        copy.start()
    pl.semaphore_wait(barrier, my_bt * pols + pols - 1)
    for b, p in everyone:

        @pl.when(my_bt > b)
        def _():
            pl.semaphore_signal(
                ready.at[me], inc=1, device_id={"bt": b, "pol": p}, device_id_type=MESH
            )

    copies[0].wait()

    mine = pl.ds(pl.multiple_of(me * slab, 8), slab)

    def post(b, p):
        t = b * pols + p

        @pl.when(my_bt < b)
        def _():
            pl.semaphore_wait(ready.at[t], 1)

        @pl.when(me != t)
        def _():
            pltpu.make_async_remote_copy(
                src_ref=send.at[pl.ds(t * slab, slab), :],
                dst_ref=recv.at[mine, :],
                send_sem=send_sem,
                recv_sem=recv_sem.at[my_bt],
                device_id={"bt": b, "pol": p},
                device_id_type=MESH,
            ).start()

    pack(gains, send, n, range(pols))
    for p in range(pols):
        post(0, p)
    pack(gains, send, n, range(pols, n))
    pltpu.make_async_copy(send.at[mine, :], recv.at[mine, :], recv_sem.at[my_bt]).start()
    for b, p in everyone[pols:]:
        post(b, p)

    pltpu.make_async_copy(stations, stations, in_sem.at[1]).wait()
    copies[3].wait()
    copies[4].wait()
    copies[5].wait()
    ck = chans * comps
    total = facets * ck
    prow = lax.broadcasted_iota(jnp.int32, (total, total), 0)
    pcol = lax.broadcasted_iota(jnp.int32, (total, total), 1)
    facet_of = pcol // ck
    dir_of = jnp.zeros_like(pcol)
    for f in range(facets):
        dir_of = jnp.where(facet_of == f, dirs[f], dir_of)
    inner = lax.rem(pcol, ck)
    seat = lax.rem(dir_of, group) * chans + inner // comps
    target = (dir_of // group * comps + lax.rem(inner, comps)) * COMPS + seat
    perm = jnp.where(prow == target, 1.0, 0.0).astype(BF16)
    flat = vis[...].astype(F32).reshape(total, rows).astype(BF16)
    planar[...] = jnp.dot(perm, flat, preferred_element_type=F32)

    tile = (COMPS, per_slot)
    col = lax.broadcasted_iota(jnp.int32, tile, 1)
    frac = (col.astype(F32) + 0.5) / per_slot
    live_rows = filled[0]
    in_low = col < HALF

    row = lax.broadcasted_iota(jnp.int32, (LANES, per_slot), 0)
    mcol = lax.broadcasted_iota(jnp.int32, (LANES, per_slot), 1)
    station = lax.rem(row, HALF)
    lower = row < HALF
    mfrac = (mcol.astype(F32) + 0.5) / per_slot
    for s in range(slots):
        now, then = 1.0 - mfrac, mfrac
        weight = jnp.where(lower, now, then) if s % 2 == 0 else jnp.where(lower, then, now)
        live = (mcol + s * per_slot) < live_rows
        lt = jnp.where((station == stations[0, s : s + 1, :]) & live, weight, 0.0)
        rt = jnp.where(station == stations[1, s : s + 1, :], weight, 0.0)
        both = jnp.concatenate([lt, rt], axis=1).astype(BF16)
        table[s, 0:LANES, :] = both
        table[s, LANES : 2 * LANES, :] = both

    for g in range(facets // group):
        for b in range(g * group // pols, -(-(g + 1) * group // pols)):
            part = recv.at[pl.ds(b * pols * slab, pols * slab), :]
            pltpu.make_async_copy(part, part, recv_sem.at[b]).wait()
        base = g * group * slab
        load = lambda at: recv[pl.ds(base + at, COMPS, stride=pitch), :]
        pairs = [[load(p * COMPS + k) for k in range(comps)] for p in range(slots // 2)]
        tails = [load(slots // 2 * COMPS + k) for k in range(comps // 2)]

        def spread(s):
            x = pairs[s // 2]
            if s % 2 == 1:
                if s + 1 < slots:
                    nxt = pairs[(s + 1) // 2]
                else:
                    nxt = [tails[k] if k < comps // 2 else pltpu.roll(tails[k - comps // 2], HALF, 1) for k in range(comps)]
                x = [jnp.where(in_low, b, a) for a, b in zip(x, nxt)]
            x = jnp.concatenate(x, axis=0)
            hi = x.astype(BF16)
            lo = (x - hi.astype(F32)).astype(BF16)
            both = jnp.dot(
                jnp.concatenate([hi, lo], axis=1), table[s], preferred_element_type=F32
            )
            cut = lambda k: slice(k * COMPS, (k + 1) * COMPS)
            return [both[cut(k), 0:per_slot] for k in range(comps)], [both[cut(k), per_slot:] for k in range(comps)]
        for s in range(slots):
            left, right = spread(s)
            data = [
                planar[(g * comps + k) * COMPS : (g * comps + k + 1) * COMPS, s * per_slot : (s + 1) * per_slot]
                for k in range(comps)
            ]
            for k, plane in enumerate(jones(left, data, right)):
                stage[s, pl.ds(g * COMPS * comps + k, COMPS, stride=comps), :] = plane

    by_dir = stage.reshape(slots, facets, ck, per_slot)
    for f in range(facets):
        for c in range(chans):
            for s in range(slots):
                out_ref[f, c, :, s * per_slot : (s + 1) * per_slot] = by_dir[
                    s, dirs[f], c * comps : (c + 1) * comps, :
                ].astype(BF16)

    sent = send.at[pl.ds(0, (n - 1) * slab), :]
    pltpu.make_async_copy(sent, sent, send_sem).wait()


def shards(gains, visibilities, first_station, second_station, filled_row_count, facet_dir):
    n = lax.axis_size(("bt", "pol"))
    pols = lax.axis_size("pol")
    facets, chans, comps, rows = visibilities.shape
    slots = GAIN_SLOT_COUNT
    slab = chans * (slots // 2 * COMPS + COMPS // 2)
    total = facets * chans * comps
    anywhere = pl.BlockSpec(memory_space=pltpu.HBM)
    return pl.pallas_call(
        functools.partial(kernel, n, pols),
        out_shape=pltpu.VMEM(visibilities.shape, BF16),
        in_specs=[anywhere] * 6,
        out_specs=pl.BlockSpec(memory_space=pltpu.VMEM),
        scratch_shapes=[
            pltpu.VMEM(gains.shape, F32),
            pltpu.VMEM(visibilities.shape, BF16),
            pltpu.VMEM((2, slots, rows // slots), jnp.int32),
            pltpu.SMEM(filled_row_count.shape, jnp.int32),
            pltpu.SMEM(facet_dir.shape, jnp.int32),
            pltpu.VMEM((n * slab, LANES), F32),
            pltpu.VMEM((n * slab, LANES), F32),
            pltpu.VMEM((total, rows), F32),
            pltpu.VMEM((slots, total, rows // slots), F32),
            pltpu.VMEM((slots, 2 * LANES, 2 * (rows // slots)), BF16),
            pltpu.SemaphoreType.DMA((5,)),
            pltpu.SemaphoreType.DMA,
            pltpu.SemaphoreType.DMA((n // pols,)),
            pltpu.SemaphoreType.REGULAR((n,)),
        ],
        compiler_params=pltpu.CompilerParams(collective_id=0, has_side_effects=True),
        name="jones",
    )(
        gains,
        visibilities,
        first_station.reshape(slots, rows // slots),
        second_station.reshape(slots, rows // slots),
        filled_row_count,
        facet_dir,
    )


def solution(mesh):
    return jax.shard_map(
        shards,
        mesh=mesh,
        in_specs=(
            P(("obs", "bt", "pol"), "freq", None, None),
            P("obs", "freq", None, ("bt", "pol")),
            P(("obs", "bt", "pol")),
            P(("obs", "bt", "pol")),
            P(("obs", "bt", "pol")),
            P("obs"),
        ),
        out_specs=P("obs", "freq", None, ("bt", "pol")),
        check_vma=False,
    )
```

time: 11.3 us -> 9.97 us (0.88)
  Pallas kernels: 9.82 us -> 8.5 us
    pallas_call x1, Pallas kernels: 9.82 us -> 8.5 us  [shards(): pl.pallas_call(functools.partial(kernel, n, pols), out_shape=pltpu.VMEM(v...]
where the time goes in v1:
time: 9.97 us; the launch traced here: 9.82 us
  Pallas kernels  8.5 us (85%)
  local copies, waits for them, and re-layouts  0.66 us (7%)
  between operations  0.66 us (7%)
    pallas_call x1, Pallas kernels, shards(): pl.pallas_call(functools.partial(kernel, n, pols), out_shape=pltpu.VMEM(v...  8.5 us
    unnamed x1, local copies, waits for them, and re-layouts  0.66 us

profile of v1, /device:TPU:0, one launch (start us, length us, event | category | flops | bytes accessed | tf_op | source)
XLA Modules:
  0.0 9.8 jit_solution(11657265391283756468)
XLA Ops:
  0.7 8.5 %jones.1 = bf16[8,2,8,512]{3,2,1,0:T(8,128)(2,1)S(1)} custom-call(f32[1,2,8,1984]{3,2,1,0:T(8,128)} %gains_hbm.1, bf16[8,2,8,512]{3,2,1,0:T(8,128)(2,1)} %vis_hbm.1, s32[4,128]{1,0:T(4,128)} %bitcast.2, s32[4,128]{1,0:T(4,128)} %bitcast.3, s32[1]{0:T(128)S(6)} %copy.9.filled_hbm, s32[8]{0:T(128)} %dir_hbm.1), custom_call_target="tpu_custom_call" | custom-call | tf_op jit(solution)/shard_map/jones/pallas_call | solution.py:272
  9.2 0.7 %copy.8 = bf16[8,2,8,512]{3,2,1,0:T(8,128)(2,1)} copy(bf16[8,2,8,512]{3,2,1,0:T(8,128)(2,1)S(1)} %jones.1) | data formatting | bytes 262144
